TPU v7x, 128 devices: a whole 4x4x4 slice. The times are simulated.
128 devices in a mesh: seq: 4 (over z_lo, core), mp: 32 (over z_hi, y, x).
Axes of the slice: x: 4, y: 4, z: 4 (z_hi: 2, z_lo: 2; z = z_hi * 2 + z_lo), core: 2. Of those that a mesh axis runs over, the one named last changes fastest.
Arguments:
- byte_states: bfloat16 [4, 16384, 1024], P('seq', 'mp'), may hold values from -312 to 312
- patch_latents: bfloat16 [4, 4096, 4096], P(None, 'seq', 'mp'), may hold values from -6 to 6
- patch_lengths: int32 [4, 4096], P('seq'), may hold values from 1 to 12, 16384 in all within a row
- w_down: bfloat16 [4096, 1024], replicated, may hold values from -0.09375 to 0.09375
- kv_gain: bfloat16 [1024], replicated, may hold values from 0.25 to 1.75
- w_query: bfloat16 [1024, 1024], replicated, may hold values from -0.375 to 0.375
- w_key: bfloat16 [1024, 1024], replicated, may hold values from -0.1875 to 0.1875
- w_value: bfloat16 [1024, 1024], replicated, may hold values from -0.1875 to 0.1875
- w_out: bfloat16 [1024, 1024], replicated, may hold values from -0.375 to 0.375
- out_gain: bfloat16 [1024], replicated, may hold values from 0.25 to 1.75
Outputs:
- decoded: bfloat16 [4, 16384, 1024], P('seq', 'mp')
Inputs may be any that keep to these rules, and one draw needn't show every extreme that they name: patch_lengths[s] lists the lengths of the 4096 patches of sequence s in order; they sum to 16384 and the longest is exactly 12.
All inputs are finite; a program needn't handle non-finite values.
Results may differ from a plain program's by a relative error of at most 0.0076.
Values may be sent and summed in bfloat16 or wider, within the bound.
No kernel may reach another device: no remote copies, remote signals or barrier semaphores. Data moves between devices by JAX's collectives and lax.ppermute only.
A program may use at most 128 MiB of HBM per device.

v0:
```python
import math
import jax
import jax.numpy as jnp
from jax import lax
from jax.sharding import PartitionSpec as P

HEADS = 16
HEAD_DIM = 64
NEG_FLOOR = -1e30


def from_partner(value, axis, apart):
    mask = 2**apart
    pairs = [(source, source ^ mask) for source in range(lax.axis_size(axis))]
    return lax.ppermute(value, axis, pairs)


def in_one_piece(arrays, axis, dim, along):
    both = jnp.concatenate(arrays, axis=along)
    filled, at, finished = (lax.all_gather(both, axis, axis=dim, tiled=True), 0, [])
    for a in arrays:
        finished.append(lax.slice_in_dim(filled, at, at + a.shape[along], axis=along))
        at += a.shape[along]
    return tuple(finished)


def rms_norm(values, gain_row):
    mean_square = jnp.mean(values * values, axis=-1, keepdims=True)
    return values * lax.rsqrt(mean_square + 1e-05) * gain_row.astype(jnp.float32)


def fold_block(fold_state, query_part, position_part, key_block, value_block, start_block):
    row_max, denominator, accumulated = fold_state
    scale_factor = 1.0 / math.sqrt(HEAD_DIM)
    scores = (
        jnp.einsum("rhd,khd->hrk", query_part, key_block, preferred_element_type=jnp.float32)
        * scale_factor
    )
    allowed = start_block[None, None, :] <= position_part[None, :, None]
    masked = jnp.where(allowed, scores, NEG_FLOOR)
    new_max = jnp.maximum(row_max, jnp.max(masked, axis=-1))
    raised = jnp.where(allowed, jnp.exp(masked - new_max[..., None]), 0.0)
    correction = jnp.exp(row_max - new_max)
    denominator = denominator * correction + jnp.sum(raised, axis=-1)
    accumulated = accumulated * correction[..., None] + jnp.einsum(
        "hrk,khd->hrd", raised.astype(jnp.bfloat16), value_block, preferred_element_type=jnp.float32
    )
    return (new_max, denominator, accumulated)


def make_folder(query_halves, position_halves, starts):

    def folder(running, arrived_piece, piece_start):
        key_piece, value_piece = arrived_piece
        piece_rows = key_piece.shape[0]
        step_rows = math.gcd(piece_rows, 512)

        def one_block(block_index, fold_state):
            offset = block_index * step_rows
            key_block = lax.dynamic_slice_in_dim(key_piece, offset, step_rows, 0).reshape(
                step_rows, HEADS, HEAD_DIM
            )
            value_block = lax.dynamic_slice_in_dim(value_piece, offset, step_rows, 0).reshape(
                step_rows, HEADS, HEAD_DIM
            )
            start_block = lax.dynamic_slice_in_dim(starts, offset, step_rows, 0)
            updated = []
            for part_index in range(2):
                part_state = tuple((member[part_index] for member in fold_state))

                def advance(inner_state, part_index=part_index):
                    return fold_block(
                        inner_state,
                        query_halves[part_index],
                        position_halves[part_index],
                        key_block,
                        value_block,
                        start_block,
                    )

                def remain(inner_state):
                    return inner_state

                needed = start_block[0] <= position_halves[part_index][-1]
                updated.append(lax.cond(needed, advance, remain, part_state))
            return tuple((jnp.stack([updated[0][slot], updated[1][slot]]) for slot in range(3)))

        return lax.fori_loop(0, piece_rows // step_rows, one_block, running)

    return folder


def per_device(
    byte_states,
    patch_latents,
    patch_lengths,
    w_down,
    kv_gain,
    w_query,
    w_key,
    w_value,
    w_out,
    out_gain,
):
    mp_count = lax.axis_size("mp")
    my_rank = lax.axis_index("mp")
    tokens_here = byte_states.shape[1]
    half_rows = tokens_here // 2
    regrouped = lax.all_to_all(
        lax.all_to_all(patch_latents, "seq", split_axis=0, concat_axis=1, tiled=True),
        "mp",
        split_axis=1,
        concat_axis=2,
        tiled=True,
    )
    projected = jnp.dot(regrouped[0], w_down, preferred_element_type=jnp.float32)
    patch_normed = rms_norm(projected, kv_gain).astype(jnp.bfloat16)
    lengths = patch_lengths[0]
    starts = jnp.cumsum(lengths) - lengths
    own_rows = byte_states[0]
    local_offsets = jnp.arange(half_rows, dtype=jnp.int32)
    first_position = my_rank * tokens_here
    top_bit = mp_count.bit_length() - 2
    partner = jnp.bitwise_xor(my_rank, mp_count // 2)
    arrived_rows = from_partner(own_rows[half_rows:], "mp", top_bit)
    work_rows = jnp.concatenate([own_rows[:half_rows], arrived_rows], axis=0)
    position_halves = jnp.stack(
        [first_position + local_offsets, partner * tokens_here + half_rows + local_offsets]
    )
    queries = jnp.dot(work_rows, w_query, preferred_element_type=jnp.float32).astype(jnp.bfloat16)
    query_halves = queries.reshape(2, half_rows, HEADS, HEAD_DIM)
    initial = (
        jnp.full((2, HEADS, half_rows), NEG_FLOOR, jnp.float32),
        jnp.zeros((2, HEADS, half_rows), jnp.float32),
        jnp.zeros((2, HEADS, half_rows, HEAD_DIM), jnp.float32),
    )
    key_rows = jnp.dot(patch_normed, w_key, preferred_element_type=jnp.float32).astype(jnp.bfloat16)
    value_rows = jnp.dot(patch_normed, w_value, preferred_element_type=jnp.float32).astype(
        jnp.bfloat16
    )
    folder = make_folder(query_halves, position_halves, starts)
    row_max, denominator, accumulated = folder(
        initial, in_one_piece((key_rows, value_rows), "mp", 0, 1), jnp.int32(0)
    )
    summed = accumulated / denominator[..., None]
    head_out = (
        jnp.transpose(summed, (0, 2, 1, 3))
        .reshape(tokens_here, HEADS * HEAD_DIM)
        .astype(jnp.bfloat16)
    )
    residual = work_rows.astype(jnp.float32) + jnp.dot(
        head_out, w_out, preferred_element_type=jnp.float32
    )
    decoded = rms_norm(residual, out_gain).astype(jnp.bfloat16)
    returned = from_partner(decoded[half_rows:], "mp", top_bit)
    decoded = jnp.concatenate([decoded[:half_rows], returned], axis=0)
    return decoded[None]


def solution(mesh):
    return jax.shard_map(
        per_device,
        mesh=mesh,
        in_specs=(
            P("seq", "mp", None),
            P(None, "seq", "mp"),
            P("seq", None),
            P(),
            P(),
            P(),
            P(),
            P(),
            P(),
            P(),
        ),
        out_specs=P("seq", "mp", None),
        check_vma=False,
    )
```

profile of v0, /device:TPU:24, one launch (start us, length us, event | category | flops | bytes accessed | tf_op | source)
XLA Modules:
  0.0 601.6 jit_solution(1319241090054931026)
XLA Ops:
  6.5 18.0 %all_to_all.27 = bf16[4,1024,128]{2,1,0:T(8,128)(2,1)S(1)} all-to-all(bf16[4,1024,128]{2,1,0:T(8,128)(2,1)} %param.17), channel_id=1, replica_groups=mesh['seq'=4,'mp'=32] {'seq'}, dimensions={0} | all-to-all | bytes 2097152 | tf_op jit(solution)/shard_map/all_to_all | solution.py:110
  24.6 17.0 %copy.45 = bf16[1,4096,128]{2,0,1:T(2,128)(2,1)} copy(bf16[1,4096,128]{2,1,0:T(8,128)(2,1)S(1)} %bitcast.101) | data formatting | bytes 2097152 | tf_op jit(solution)/shard_map/all_to_all | solution.py:110
  42.1 23.4 %reduce.2 = bf16[4096,128]{1,0:T(8,128)(2,1)S(1)} reduce(bf16[4096,1,128]{2,1,0:T(2,128)(2,1)} %bitcast.98, bf16[]{:T(256)} %broadcast.104), dimensions={1}, to_apply=%bitcast.78.reduce_sub_computation | reduce | bytes 2097154
  66.7 10.6 %all-to-all-start.1 = ((bf16[32,2,8192]{2,1,0:T(2,128)(2,1)}), bf16[32,2,8192]{2,1,0:T(2,128)(2,1)S(1)}, u32[]{:S(2)}, u32[]{:S(2)}) async-start(bf16[32,2,8192]{2,1,0:T(2,128)(2,1)} %reshape.140), calls=%async_computation.1 | async-start | bytes 2097152 | tf_op jit(solution)/shard_map/all_to_all | solution.py:109
  77.5 16.8 %all-to-all-done.1 = bf16[32,2,8192]{2,1,0:T(2,128)(2,1)S(1)} async-done(((bf16[32,2,8192]{2,1,0:T(2,128)(2,1)}), bf16[32,2,8192]{2,1,0:T(2,128)(2,1)S(1)}, u32[]{:S(2)}, u32[]{:S(2)}) %all-to-all-start.1) | async-done | bytes 1048608 | tf_op jit(solution)/shard_map/all_to_all | solution.py:109
  94.4 3.5 reshape.141
  102.2 4.9 multiply_reduce_fusion.1
  112.3 15.8 %collective-permute-done = bf16[256,1024]{1,0:T(8,128)(2,1)S(1)} collective-permute-done((bf16[256,1024]{1,0:T(8,128)(2,1)}, bf16[256,1024]{1,0:T(8,128)(2,1)S(1)}, u32[]{:S(2)}, u32[]{:S(2)}) %collective-permute-start) | collective-permute-done | bytes 524320 | tf_op jit(solution)/shard_map/ppermute | solution.py:15
  128.1 4.0 convolution_convert_fusion
  132.1 4.0 reshape.138
  136.1 3.5 copy.36
  139.6 123.1 %all-gather.2.cloned.1.call-done = bf16[4096,2048]{1,0:T(8,128)(2,1)} async-done(((bf16[128,2048]{1,0:T(8,128)(2,1)}), bf16[4096,2048]{1,0:T(8,128)(2,1)}) %all-gather.2.cloned.1.call-update) | async-done | bytes 16777232 | tf_op jit(solution)/shard_map/all_gather | solution.py:20
  262.7 11.6 %fusion.38 = (bf16[4096,1024]{1,0:T(8,128)(2,1)}, bf16[4096,1024]{1,0:T(8,128)(2,1)}) fusion(bf16[4096,2048]{1,0:T(8,128)(2,1)} %all-gather.2.cloned.1.call-done), kind=kLoop, calls=%fused_computation.69 | loop fusion | bytes 33554432 | tf_op jit(solution)/shard_map/slice | solution.py:22
  275.9 297.0 %while.17 = (s32[]{:T(128)}, f32[2,16,256]{2,1,0:T(8,128)S(1)}, f32[2,16,256]{2,1,0:T(8,128)S(1)}, f32[2,16,256,64]{2,3,1,0:T(8,128)}, s32[4096]{0:T(1024)S(1)},...) while((s32[]{:T(128)}, f32[2,16,256]{2,1,0:T(8,128)S(1)}, ...), condition=%wide.region_12.13_spmd, body=%wide.region_3.12_spmd.sunk | while | flops 1130135552 | bytes 99363408 | solution.py:88
  289.4 10.8 %conditional.5 = (f32[1,16,256]{2,1,0:T(8,128)}, f32[1,16,256]{2,1,0:T(8,128)S(1)}, f32[1,16,256,64]{2,3,1,0:T(8,128)S(1)}) conditional(s32[]{:T(128)} %bitcast.90, (f32[16,256]{1,0:T(8,128)}, f32[16,256]{1,0:T(8,128)S(1)}, f32[16,256,64]{1,2,0:T(8,128)S(1)}) %tuple.134, (s32[512]{0:T(512)S(1)}, s32[256]{0:T(256)S(1)}, ...), branch_computations={%region_4.4_spmd, %region_5.0_spmd} | conditional | flops 564797440 | bytes 34835508 | solution.py:85
  302.8 11.9 %conditional.4 = (f32[1,16,256]{2,1,0:T(8,128)}, f32[1,16,256]{2,1,0:T(8,128)S(1)}, f32[1,16,256,64]{2,3,1,0:T(8,128)}) conditional(s32[]{:T(128)} %bitcast.87, (f32[16,256]{1,0:T(8,128)}, f32[16,256]{1,0:T(8,128)S(1)}, f32[16,256,64]{1,2,0:T(8,128)}) %tuple.132, (s32[512]{0:T(512)S(1)}, s32[256]{0:T(256)S(1)}, bf16[2,256,16,64]{1,3,2,0:T(8,128)(2,1)}, ...), branch_computations={%region_8.8_spmd, %region_9.0_spmd} | conditional | flops 564797440 | bytes 43224172 | solution.py:85
  306.5 3.2 fusion.20
  331.9 10.8 %conditional.5 = (f32[1,16,256]{2,1,0:T(8,128)}, f32[1,16,256]{2,1,0:T(8,128)S(1)}, f32[1,16,256,64]{2,3,1,0:T(8,128)S(1)}) conditional(s32[]{:T(128)} %bitcast.90, (f32[16,256]{1,0:T(8,128)}, f32[16,256]{1,0:T(8,128)S(1)}, f32[16,256,64]{1,2,0:T(8,128)S(1)}) %tuple.134, (s32[512]{0:T(512)S(1)}, s32[256]{0:T(256)S(1)}, ...), branch_computations={%region_4.4_spmd, %region_5.0_spmd} | conditional | flops 564797440 | bytes 34835508 | solution.py:85
  335.6 3.2 fusion.2
  345.3 11.9 %conditional.4 = (f32[1,16,256]{2,1,0:T(8,128)}, f32[1,16,256]{2,1,0:T(8,128)S(1)}, f32[1,16,256,64]{2,3,1,0:T(8,128)}) conditional(s32[]{:T(128)} %bitcast.87, (f32[16,256]{1,0:T(8,128)}, f32[16,256]{1,0:T(8,128)S(1)}, f32[16,256,64]{1,2,0:T(8,128)}) %tuple.132, (s32[512]{0:T(512)S(1)}, s32[256]{0:T(256)S(1)}, bf16[2,256,16,64]{1,3,2,0:T(8,128)(2,1)}, ...), branch_computations={%region_8.8_spmd, %region_9.0_spmd} | conditional | flops 564797440 | bytes 43224172 | solution.py:85
  349.0 3.2 fusion.20
  374.4 10.8 %conditional.5 = (f32[1,16,256]{2,1,0:T(8,128)}, f32[1,16,256]{2,1,0:T(8,128)S(1)}, f32[1,16,256,64]{2,3,1,0:T(8,128)S(1)}) conditional(s32[]{:T(128)} %bitcast.90, (f32[16,256]{1,0:T(8,128)}, f32[16,256]{1,0:T(8,128)S(1)}, f32[16,256,64]{1,2,0:T(8,128)S(1)}) %tuple.134, (s32[512]{0:T(512)S(1)}, s32[256]{0:T(256)S(1)}, ...), branch_computations={%region_4.4_spmd, %region_5.0_spmd} | conditional | flops 564797440 | bytes 34835508 | solution.py:85
  387.8 11.9 %conditional.4 = (f32[1,16,256]{2,1,0:T(8,128)}, f32[1,16,256]{2,1,0:T(8,128)S(1)}, f32[1,16,256,64]{2,3,1,0:T(8,128)}) conditional(s32[]{:T(128)} %bitcast.87, (f32[16,256]{1,0:T(8,128)}, f32[16,256]{1,0:T(8,128)S(1)}, f32[16,256,64]{1,2,0:T(8,128)}) %tuple.132, (s32[512]{0:T(512)S(1)}, s32[256]{0:T(256)S(1)}, bf16[2,256,16,64]{1,3,2,0:T(8,128)(2,1)}, ...), branch_computations={%region_8.8_spmd, %region_9.0_spmd} | conditional | flops 564797440 | bytes 43224172 | solution.py:85
  416.9 10.8 %conditional.5 = (f32[1,16,256]{2,1,0:T(8,128)}, f32[1,16,256]{2,1,0:T(8,128)S(1)}, f32[1,16,256,64]{2,3,1,0:T(8,128)S(1)}) conditional(s32[]{:T(128)} %bitcast.90, (f32[16,256]{1,0:T(8,128)}, f32[16,256]{1,0:T(8,128)S(1)}, f32[16,256,64]{1,2,0:T(8,128)S(1)}) %tuple.134, (s32[512]{0:T(512)S(1)}, s32[256]{0:T(256)S(1)}, ...), branch_computations={%region_4.4_spmd, %region_5.0_spmd} | conditional | flops 564797440 | bytes 34835508 | solution.py:85
  420.6 3.2 fusion.2
  430.3 11.9 %conditional.4 = (f32[1,16,256]{2,1,0:T(8,128)}, f32[1,16,256]{2,1,0:T(8,128)S(1)}, f32[1,16,256,64]{2,3,1,0:T(8,128)}) conditional(s32[]{:T(128)} %bitcast.87, (f32[16,256]{1,0:T(8,128)}, f32[16,256]{1,0:T(8,128)S(1)}, f32[16,256,64]{1,2,0:T(8,128)}) %tuple.132, (s32[512]{0:T(512)S(1)}, s32[256]{0:T(256)S(1)}, bf16[2,256,16,64]{1,3,2,0:T(8,128)(2,1)}, ...), branch_computations={%region_8.8_spmd, %region_9.0_spmd} | conditional | flops 564797440 | bytes 43224172 | solution.py:85
  434.0 3.2 fusion.20
  462.0 11.9 %conditional.4 = (f32[1,16,256]{2,1,0:T(8,128)}, f32[1,16,256]{2,1,0:T(8,128)S(1)}, f32[1,16,256,64]{2,3,1,0:T(8,128)}) conditional(s32[]{:T(128)} %bitcast.87, (f32[16,256]{1,0:T(8,128)}, f32[16,256]{1,0:T(8,128)S(1)}, f32[16,256,64]{1,2,0:T(8,128)}) %tuple.132, (s32[512]{0:T(512)S(1)}, s32[256]{0:T(256)S(1)}, bf16[2,256,16,64]{1,3,2,0:T(8,128)(2,1)}, ...), branch_computations={%region_8.8_spmd, %region_9.0_spmd} | conditional | flops 564797440 | bytes 43224172 | solution.py:85
  493.7 11.9 %conditional.4 = (f32[1,16,256]{2,1,0:T(8,128)}, f32[1,16,256]{2,1,0:T(8,128)S(1)}, f32[1,16,256,64]{2,3,1,0:T(8,128)}) conditional(s32[]{:T(128)} %bitcast.87, (f32[16,256]{1,0:T(8,128)}, f32[16,256]{1,0:T(8,128)S(1)}, f32[16,256,64]{1,2,0:T(8,128)}) %tuple.132, (s32[512]{0:T(512)S(1)}, s32[256]{0:T(256)S(1)}, bf16[2,256,16,64]{1,3,2,0:T(8,128)(2,1)}, ...), branch_computations={%region_8.8_spmd, %region_9.0_spmd} | conditional | flops 564797440 | bytes 43224172 | solution.py:85
  525.5 11.9 %conditional.4 = (f32[1,16,256]{2,1,0:T(8,128)}, f32[1,16,256]{2,1,0:T(8,128)S(1)}, f32[1,16,256,64]{2,3,1,0:T(8,128)}) conditional(s32[]{:T(128)} %bitcast.87, (f32[16,256]{1,0:T(8,128)}, f32[16,256]{1,0:T(8,128)S(1)}, f32[16,256,64]{1,2,0:T(8,128)}) %tuple.132, (s32[512]{0:T(512)S(1)}, s32[256]{0:T(256)S(1)}, bf16[2,256,16,64]{1,3,2,0:T(8,128)(2,1)}, ...), branch_computations={%region_8.8_spmd, %region_9.0_spmd} | conditional | flops 564797440 | bytes 43224172 | solution.py:85
  557.2 11.9 %conditional.4 = (f32[1,16,256]{2,1,0:T(8,128)}, f32[1,16,256]{2,1,0:T(8,128)S(1)}, f32[1,16,256,64]{2,3,1,0:T(8,128)}) conditional(s32[]{:T(128)} %bitcast.87, (f32[16,256]{1,0:T(8,128)}, f32[16,256]{1,0:T(8,128)S(1)}, f32[16,256,64]{1,2,0:T(8,128)}) %tuple.132, (s32[512]{0:T(512)S(1)}, s32[256]{0:T(256)S(1)}, bf16[2,256,16,64]{1,3,2,0:T(8,128)(2,1)}, ...), branch_computations={%region_8.8_spmd, %region_9.0_spmd} | conditional | flops 564797440 | bytes 43224172 | solution.py:85
  579.3 14.4 %collective-permute-done.1 = bf16[256,1024]{1,0:T(8,128)(2,1)S(1)} collective-permute-done((bf16[256,1024]{1,0:T(8,128)(2,1)S(1)}, bf16[256,1024]{1,0:T(8,128)(2,1)S(1)}, u32[]{:S(2)}, u32[]{:S(2)}) %collective-permute-start.1) | collective-permute-done | bytes 524320 | tf_op jit(solution)/shard_map/ppermute | solution.py:15
  (307 shorter events, 279.6 us)
Async XLA Ops:
  6.5 569.6 %copy-start = (bf16[1024,1024]{1,0:T(8,128)(2,1)S(1)}, bf16[1024,1024]{1,0:T(8,128)(2,1)}, u32[]{:S(2)}) copy-start(bf16[1024,1024]{1,0:T(8,128)(2,1)} %param.24) | copy-start | bytes 6291460
  6.5 71.0 %copy-start.13 = (bf16[1024]{0:T(1024)(128)(2,1)S(1)}, bf16[1024]{0:T(1024)(128)(2,1)}, u32[]{:S(2)}) copy-start(bf16[1024]{0:T(1024)(128)(2,1)} %param.20) | copy-start | bytes 6148
  66.7 27.7 %all-to-all-start.1 = ((bf16[32,2,8192]{2,1,0:T(2,128)(2,1)}), bf16[32,2,8192]{2,1,0:T(2,128)(2,1)S(1)}, u32[]{:S(2)}, u32[]{:S(2)}) async-start(bf16[32,2,8192]{2,1,0:T(2,128)(2,1)} %reshape.140), calls=%async_computation.1 | async-start | bytes 2097152 | tf_op jit(solution)/shard_map/all_to_all | solution.py:109
  77.3 185.4 %all-gather.2.cloned.1.call-start = ((), (), s32[]{:S(2)}) async-start(), calls=%async_computation.2 | async-start | bytes 17301504 | tf_op jit(solution)/shard_map/all_gather | solution.py:20
  102.2 5.0 copy-start.10
  102.2 5.5 copy-start.11
  111.1 28.5 %copy-start.6 = (bf16[256,1024]{1,0:T(8,128)(2,1)}, bf16[256,1024]{1,0:T(8,128)(2,1)S(1)}, u32[]{:S(2)}) copy-start(bf16[256,1024]{1,0:T(8,128)(2,1)S(1)} %get-tuple-element.383) | copy-start | bytes 1572868
  111.1 17.0 %collective-permute-start = (bf16[256,1024]{1,0:T(8,128)(2,1)}, bf16[256,1024]{1,0:T(8,128)(2,1)S(1)}, u32[]{:S(2)}, u32[]{:S(2)}) collective-permute-start(bf16[256,1024]{1,0:T(8,128)(2,1)} %get-tuple-element.384), channel_id=1, source_target_pairs={{0,16},{1,17},{2,18},{3,19},{4,20},{5,21},{6,22},{7,23},{8,24},{9,... | collective-permute-start | bytes 1572872 | tf_op jit(solution)/shard_map/ppermute | solution.py:15
  128.1 146.3 %copy-start.8 = (bf16[256,1024]{1,0:T(8,128)(2,1)}, bf16[256,1024]{1,0:T(8,128)(2,1)S(1)}, u32[]{:S(2)}) copy-start(bf16[256,1024]{1,0:T(8,128)(2,1)S(1)} %collective-permute-done) | copy-start | bytes 1572868
  289.6 7.5 %copy-start.4 = (bf16[512,16,64]{0,2,1:T(8,128)(2,1)S(1)}, bf16[512,16,64]{0,2,1:T(8,128)(2,1)}, u32[]{:S(2)}) copy-start(bf16[512,16,64]{0,2,1:T(8,128)(2,1)} %get-tuple-element.249) | copy-start | bytes 3145732 | tf_op jit(solution)/shard_map/while/body/eval_jaxpr/cond
  302.9 7.5 %copy-start.1 = (f32[16,256,64]{1,2,0:T(8,128)S(1)}, f32[16,256,64]{1,2,0:T(8,128)}, u32[]{:S(2)}) copy-start(f32[16,256,64]{1,2,0:T(8,128)} %get-tuple-element.256) | copy-start | bytes 3145732 | tf_op jit(solution)/shard_map/while/body/eval_jaxpr/cond
  302.9 7.5 %copy-start.5 = (bf16[512,16,64]{0,2,1:T(8,128)(2,1)S(1)}, bf16[512,16,64]{0,2,1:T(8,128)(2,1)}, u32[]{:S(2)}) copy-start(bf16[512,16,64]{0,2,1:T(8,128)(2,1)} %get-tuple-element.257) | copy-start | bytes 3145732 | tf_op jit(solution)/shard_map/while/body/eval_jaxpr/cond
  332.1 7.5 %copy-start.4 = (bf16[512,16,64]{0,2,1:T(8,128)(2,1)S(1)}, bf16[512,16,64]{0,2,1:T(8,128)(2,1)}, u32[]{:S(2)}) copy-start(bf16[512,16,64]{0,2,1:T(8,128)(2,1)} %get-tuple-element.249) | copy-start | bytes 3145732 | tf_op jit(solution)/shard_map/while/body/eval_jaxpr/cond
  345.4 7.5 %copy-start.1 = (f32[16,256,64]{1,2,0:T(8,128)S(1)}, f32[16,256,64]{1,2,0:T(8,128)}, u32[]{:S(2)}) copy-start(f32[16,256,64]{1,2,0:T(8,128)} %get-tuple-element.256) | copy-start | bytes 3145732 | tf_op jit(solution)/shard_map/while/body/eval_jaxpr/cond
  345.4 7.5 %copy-start.5 = (bf16[512,16,64]{0,2,1:T(8,128)(2,1)S(1)}, bf16[512,16,64]{0,2,1:T(8,128)(2,1)}, u32[]{:S(2)}) copy-start(bf16[512,16,64]{0,2,1:T(8,128)(2,1)} %get-tuple-element.257) | copy-start | bytes 3145732 | tf_op jit(solution)/shard_map/while/body/eval_jaxpr/cond
  374.6 7.5 %copy-start.4 = (bf16[512,16,64]{0,2,1:T(8,128)(2,1)S(1)}, bf16[512,16,64]{0,2,1:T(8,128)(2,1)}, u32[]{:S(2)}) copy-start(bf16[512,16,64]{0,2,1:T(8,128)(2,1)} %get-tuple-element.249) | copy-start | bytes 3145732 | tf_op jit(solution)/shard_map/while/body/eval_jaxpr/cond
  387.9 7.5 %copy-start.1 = (f32[16,256,64]{1,2,0:T(8,128)S(1)}, f32[16,256,64]{1,2,0:T(8,128)}, u32[]{:S(2)}) copy-start(f32[16,256,64]{1,2,0:T(8,128)} %get-tuple-element.256) | copy-start | bytes 3145732 | tf_op jit(solution)/shard_map/while/body/eval_jaxpr/cond
  387.9 7.5 %copy-start.5 = (bf16[512,16,64]{0,2,1:T(8,128)(2,1)S(1)}, bf16[512,16,64]{0,2,1:T(8,128)(2,1)}, u32[]{:S(2)}) copy-start(bf16[512,16,64]{0,2,1:T(8,128)(2,1)} %get-tuple-element.257) | copy-start | bytes 3145732 | tf_op jit(solution)/shard_map/while/body/eval_jaxpr/cond
  417.1 7.5 %copy-start.4 = (bf16[512,16,64]{0,2,1:T(8,128)(2,1)S(1)}, bf16[512,16,64]{0,2,1:T(8,128)(2,1)}, u32[]{:S(2)}) copy-start(bf16[512,16,64]{0,2,1:T(8,128)(2,1)} %get-tuple-element.249) | copy-start | bytes 3145732 | tf_op jit(solution)/shard_map/while/body/eval_jaxpr/cond
  430.4 7.5 %copy-start.1 = (f32[16,256,64]{1,2,0:T(8,128)S(1)}, f32[16,256,64]{1,2,0:T(8,128)}, u32[]{:S(2)}) copy-start(f32[16,256,64]{1,2,0:T(8,128)} %get-tuple-element.256) | copy-start | bytes 3145732 | tf_op jit(solution)/shard_map/while/body/eval_jaxpr/cond
  430.4 7.5 %copy-start.5 = (bf16[512,16,64]{0,2,1:T(8,128)(2,1)S(1)}, bf16[512,16,64]{0,2,1:T(8,128)(2,1)}, u32[]{:S(2)}) copy-start(bf16[512,16,64]{0,2,1:T(8,128)(2,1)} %get-tuple-element.257) | copy-start | bytes 3145732 | tf_op jit(solution)/shard_map/while/body/eval_jaxpr/cond
  462.2 7.5 %copy-start.1 = (f32[16,256,64]{1,2,0:T(8,128)S(1)}, f32[16,256,64]{1,2,0:T(8,128)}, u32[]{:S(2)}) copy-start(f32[16,256,64]{1,2,0:T(8,128)} %get-tuple-element.256) | copy-start | bytes 3145732 | tf_op jit(solution)/shard_map/while/body/eval_jaxpr/cond
  462.2 7.5 %copy-start.5 = (bf16[512,16,64]{0,2,1:T(8,128)(2,1)S(1)}, bf16[512,16,64]{0,2,1:T(8,128)(2,1)}, u32[]{:S(2)}) copy-start(bf16[512,16,64]{0,2,1:T(8,128)(2,1)} %get-tuple-element.257) | copy-start | bytes 3145732 | tf_op jit(solution)/shard_map/while/body/eval_jaxpr/cond
  493.9 7.5 %copy-start.1 = (f32[16,256,64]{1,2,0:T(8,128)S(1)}, f32[16,256,64]{1,2,0:T(8,128)}, u32[]{:S(2)}) copy-start(f32[16,256,64]{1,2,0:T(8,128)} %get-tuple-element.256) | copy-start | bytes 3145732 | tf_op jit(solution)/shard_map/while/body/eval_jaxpr/cond
  493.9 7.5 %copy-start.5 = (bf16[512,16,64]{0,2,1:T(8,128)(2,1)S(1)}, bf16[512,16,64]{0,2,1:T(8,128)(2,1)}, u32[]{:S(2)}) copy-start(bf16[512,16,64]{0,2,1:T(8,128)(2,1)} %get-tuple-element.257) | copy-start | bytes 3145732 | tf_op jit(solution)/shard_map/while/body/eval_jaxpr/cond
  525.6 7.5 %copy-start.1 = (f32[16,256,64]{1,2,0:T(8,128)S(1)}, f32[16,256,64]{1,2,0:T(8,128)}, u32[]{:S(2)}) copy-start(f32[16,256,64]{1,2,0:T(8,128)} %get-tuple-element.256) | copy-start | bytes 3145732 | tf_op jit(solution)/shard_map/while/body/eval_jaxpr/cond
  525.6 7.5 %copy-start.5 = (bf16[512,16,64]{0,2,1:T(8,128)(2,1)S(1)}, bf16[512,16,64]{0,2,1:T(8,128)(2,1)}, u32[]{:S(2)}) copy-start(bf16[512,16,64]{0,2,1:T(8,128)(2,1)} %get-tuple-element.257) | copy-start | bytes 3145732 | tf_op jit(solution)/shard_map/while/body/eval_jaxpr/cond
  557.4 7.5 %copy-start.1 = (f32[16,256,64]{1,2,0:T(8,128)S(1)}, f32[16,256,64]{1,2,0:T(8,128)}, u32[]{:S(2)}) copy-start(f32[16,256,64]{1,2,0:T(8,128)} %get-tuple-element.256) | copy-start | bytes 3145732 | tf_op jit(solution)/shard_map/while/body/eval_jaxpr/cond
  557.4 7.5 %copy-start.5 = (bf16[512,16,64]{0,2,1:T(8,128)(2,1)S(1)}, bf16[512,16,64]{0,2,1:T(8,128)(2,1)}, u32[]{:S(2)}) copy-start(bf16[512,16,64]{0,2,1:T(8,128)(2,1)} %get-tuple-element.257) | copy-start | bytes 3145732 | tf_op jit(solution)/shard_map/while/body/eval_jaxpr/cond
  572.9 5.9 copy-start.7
  572.9 5.9 copy-start.9
  579.2 14.5 %collective-permute-start.1 = (bf16[256,1024]{1,0:T(8,128)(2,1)S(1)}, bf16[256,1024]{1,0:T(8,128)(2,1)S(1)}, u32[]{:S(2)}, u32[]{:S(2)}) collective-permute-start(bf16[256,1024]{1,0:T(8,128)(2,1)S(1)} %get-tuple-element.382), channel_id=1, source_target_pairs={{0,16},{1,17},{2,18},{3,19},{4,20},{5,21},{6,22},{7,23},{8,24},{9,... | collective-permute-start | bytes 1572872 | tf_op jit(solution)/shard_map/ppermute | solution.py:15
  (18 other events, 37.8 us)
Sparse Core Ops, SparseCore 0:
  109.2 153.5 all-gather.1
where the time goes:
time: 608 us; the launch traced here: 602 us
  waiting for transfers between devices  170 us (28%)
  local copies, waits for them, and re-layouts  167 us (27%)
  other arithmetic  115 us (19%)
  matrix products  85.1 us (14%)
  loops' own time  21.4 us (4%)
  blocking collectives  18 us (3%)
  between operations  13.6 us (2%)
  starting transfers between devices  11.5 us (2%)
    all_gather x1, waiting for transfers between devices, in_one_piece(): lax.all_gather(both, axis, axis=dim, tiled=True)  123 us
    dynamic_slice x16, local copies, waits for them, and re-layouts, one_block(): lax.dynamic_slice_in_dim(value_piece, offset, step_rows, 0)  42.7 us
    another operation x36, other arithmetic, one_block(): jnp.stack([updated[0][slot], updated[1][slot]])  39.4 us
    reduce_sum x12, other arithmetic, fold_block(): denominator = denominator * correction + jnp.sum(raised, axis=-1)  38.8 us
    dot_general x12, matrix products, fold_block(): jnp.einsum('hrk,khd->hrd', raised.astype(jnp.bfloat16), value_block, pref...  37.8 us
    dot_general x12, matrix products, fold_block(): jnp.einsum('rhd,khd->hrk', query_part, key_block, preferred_element_type=...  34.8 us
    ppermute x2, waiting for transfers between devices, from_partner(): return lax.ppermute(value, axis, pairs)  30.2 us
    squeeze x16, local copies, waits for them, and re-layouts, one_block(): part_state = tuple((member[part_index] for member in fold_state))  26.5 us
  transfers between devices with their start and end apart: 4, of which 4 were waited for; matrix products, arithmetic and copies ran while one was open for 2% of the time, Pallas kernels for 0%

commit v1 on v0

--- a/solution.py
+++ b/solution.py
@@ -106,12 +106,20 @@
     my_rank = lax.axis_index("mp")
     tokens_here = byte_states.shape[1]
     half_rows = tokens_here // 2
-    regrouped = lax.all_to_all(
-        lax.all_to_all(patch_latents, "seq", split_axis=0, concat_axis=1, tiled=True),
-        "mp",
-        split_axis=1,
-        concat_axis=2,
-        tiled=True,
+    regrouped = jnp.concatenate(
+        lax.all_to_all(
+            jnp.stack(
+                jnp.split(
+                    lax.all_to_all(patch_latents, "seq", split_axis=0, concat_axis=1, tiled=True),
+                    lax.axis_size("mp"),
+                    axis=1,
+                )
+            ),
+            "mp",
+            0,
+            0,
+        ),
+        axis=2,
     )
     projected = jnp.dot(regrouped[0], w_down, preferred_element_type=jnp.float32)
     patch_normed = rms_norm(projected, kv_gain).astype(jnp.bfloat16)

time: 608 us -> 581 us (0.956)
  other arithmetic: 115 us -> 92 us
    unnamed x1 -> x0, other arithmetic: 23.4 us -> none
    all_to_all x2 -> x0, local copies, waits for them, and re-layouts: 18.6 us -> none  [the longest x1 17 us: per_device(): lax.all_to_all(patch_latents, 'seq', split_axis=0, concat_axis=1, tiled=T...]
    unnamed x25 -> x84, local copies, waits for them, and re-layouts: 8.08 us -> 23.3 us
where the time goes in v1:
time: 581 us; the launch traced here: 575 us
  waiting for transfers between devices  170 us (29%)
  local copies, waits for them, and re-layouts  164 us (28%)
  other arithmetic  92 us (16%)
  matrix products  85.1 us (15%)
  loops' own time  20.5 us (4%)
  blocking collectives  18 us (3%)
  between operations  13.8 us (2%)
  starting transfers between devices  11.3 us (2%)
    all_gather x1, waiting for transfers between devices, in_one_piece(): lax.all_gather(both, axis, axis=dim, tiled=True)  123 us
    dynamic_slice x16, local copies, waits for them, and re-layouts, one_block(): lax.dynamic_slice_in_dim(value_piece, offset, step_rows, 0)  42.7 us
    another operation x36, other arithmetic, one_block(): jnp.stack([updated[0][slot], updated[1][slot]])  39.5 us
    reduce_sum x12, other arithmetic, fold_block(): denominator = denominator * correction + jnp.sum(raised, axis=-1)  38.8 us
    dot_general x12, matrix products, fold_block(): jnp.einsum('hrk,khd->hrd', raised.astype(jnp.bfloat16), value_block, pref...  37.8 us
    dot_general x12, matrix products, fold_block(): jnp.einsum('rhd,khd->hrk', query_part, key_block, preferred_element_type=...  34.8 us
    ppermute x2, waiting for transfers between devices, from_partner(): return lax.ppermute(value, axis, pairs)  30.2 us
    squeeze x16, local copies, waits for them, and re-layouts, one_block(): part_state = tuple((member[part_index] for member in fold_state))  26.7 us
  transfers between devices with their start and end apart: 4, of which 4 were waited for; matrix products, arithmetic and copies ran while one was open for 2% of the time, Pallas kernels for 0%

profile of v1, /device:TPU:24, one launch (start us, length us, event | category | flops | bytes accessed | tf_op | source)
XLA Modules:
  0.0 575.0 jit_solution(6680212217001976158)
XLA Ops:
  6.5 18.0 %all_to_all.17 = bf16[4,1024,128]{2,1,0:T(8,128)(2,1)S(1)} all-to-all(bf16[4,1024,128]{2,1,0:T(8,128)(2,1)} %param.17), channel_id=1, replica_groups=mesh['seq'=4,'mp'=32] {'seq'}, dimensions={0} | all-to-all | bytes 2097152 | tf_op jit(solution)/shard_map/all_to_all | solution.py:113
  48.5 10.6 %all-to-all-start.1 = ((bf16[32,1,128,128]{2,3,1,0:T(8,128)(2,1)}), bf16[32,1,128,128]{2,3,1,0:T(8,128)(2,1)S(1)}, u32[]{:S(2)}, u32[]{:S(2)}) async-start(bf16[32,1,128,128]{2,3,1,0:T(8,128)(2,1)} %constant_dynamic-update-slice_fusion), calls=%async_computation.1 | async-start | bytes 2097152 | tf_op jit(solution)/shard_map/all_to_all | solution.py:110
  59.2 17.0 %all-to-all-done.1 = bf16[32,1,128,128]{2,3,1,0:T(8,128)(2,1)S(1)} async-done(((bf16[32,1,128,128]{2,3,1,0:T(8,128)(2,1)}), bf16[32,1,128,128]{2,3,1,0:T(8,128)(2,1)S(1)}, u32[]{:S(2)}, u32[]{:S(2)}) %all-to-all-start.1) | async-done | bytes 1048608 | tf_op jit(solution)/shard_map/all_to_all | solution.py:110
  76.2 4.9 multiply_reduce_fusion.1
  86.3 15.8 %collective-permute-done = bf16[256,1024]{1,0:T(8,128)(2,1)S(1)} collective-permute-done((bf16[256,1024]{1,0:T(8,128)(2,1)}, bf16[256,1024]{1,0:T(8,128)(2,1)S(1)}, u32[]{:S(2)}, u32[]{:S(2)}) %collective-permute-start) | collective-permute-done | bytes 524320 | tf_op jit(solution)/shard_map/ppermute | solution.py:15
  102.1 4.0 convolution_convert_fusion
  106.1 4.0 reshape.141
  110.1 3.5 copy.56
  113.6 123.1 %all-gather.2.cloned.1.call-done = bf16[4096,2048]{1,0:T(8,128)(2,1)} async-done(((bf16[128,2048]{1,0:T(8,128)(2,1)}), bf16[4096,2048]{1,0:T(8,128)(2,1)}) %all-gather.2.cloned.1.call-update) | async-done | bytes 16777232 | tf_op jit(solution)/shard_map/all_gather | solution.py:20
  236.7 11.6 %fusion.38 = (bf16[4096,1024]{1,0:T(8,128)(2,1)}, bf16[4096,1024]{1,0:T(8,128)(2,1)}) fusion(bf16[4096,2048]{1,0:T(8,128)(2,1)} %all-gather.2.cloned.1.call-done), kind=kLoop, calls=%fused_computation.101 | loop fusion | bytes 33554432 | tf_op jit(solution)/shard_map/slice | solution.py:22
  250.0 296.3 %while.17 = (s32[]{:T(128)}, f32[2,16,256]{2,1,0:T(8,128)S(1)}, f32[2,16,256]{2,1,0:T(8,128)S(1)}, f32[2,16,256,64]{2,3,1,0:T(8,128)}, s32[4096]{0:T(1024)S(1)},...) while((s32[]{:T(128)}, f32[2,16,256]{2,1,0:T(8,128)S(1)}, ...), condition=%wide.region_12.13_spmd, body=%wide.region_3.12_spmd.sunk | while | flops 1130135552 | bytes 99363408 | solution.py:88
  263.2 10.8 %conditional.5 = (f32[1,16,256]{2,1,0:T(8,128)}, f32[1,16,256]{2,1,0:T(8,128)S(1)}, f32[1,16,256,64]{2,3,1,0:T(8,128)S(1)}) conditional(s32[]{:T(128)} %bitcast.151, (f32[16,256]{1,0:T(8,128)}, f32[16,256]{1,0:T(8,128)S(1)}, f32[16,256,64]{1,2,0:T(8,128)S(1)}) %tuple.162, (s32[512]{0:T(512)S(1)}, s32[256]{0:T(256)S(1)}, ...), branch_computations={%region_4.4_spmd, %region_5.0_spmd} | conditional | flops 564797440 | bytes 34835508 | solution.py:85
  266.9 3.2 fusion.2
  276.7 11.9 %conditional.4 = (f32[1,16,256]{2,1,0:T(8,128)}, f32[1,16,256]{2,1,0:T(8,128)S(1)}, f32[1,16,256,64]{2,3,1,0:T(8,128)}) conditional(s32[]{:T(128)} %bitcast.148, (f32[16,256]{1,0:T(8,128)}, f32[16,256]{1,0:T(8,128)S(1)}, f32[16,256,64]{1,2,0:T(8,128)}) %tuple.160, (s32[512]{0:T(512)S(1)}, s32[256]{0:T(256)S(1)}, bf16[2,256,16,64]{1,3,2,0:T(8,128)(2,1)}, ...), branch_computations={%region_8.8_spmd, %region_9.0_spmd} | conditional | flops 564797440 | bytes 43224172 | solution.py:85
  305.7 10.8 %conditional.5 = (f32[1,16,256]{2,1,0:T(8,128)}, f32[1,16,256]{2,1,0:T(8,128)S(1)}, f32[1,16,256,64]{2,3,1,0:T(8,128)S(1)}) conditional(s32[]{:T(128)} %bitcast.151, (f32[16,256]{1,0:T(8,128)}, f32[16,256]{1,0:T(8,128)S(1)}, f32[16,256,64]{1,2,0:T(8,128)S(1)}) %tuple.162, (s32[512]{0:T(512)S(1)}, s32[256]{0:T(256)S(1)}, ...), branch_computations={%region_4.4_spmd, %region_5.0_spmd} | conditional | flops 564797440 | bytes 34835508 | solution.py:85
  309.3 3.2 fusion.2
  319.1 11.9 %conditional.4 = (f32[1,16,256]{2,1,0:T(8,128)}, f32[1,16,256]{2,1,0:T(8,128)S(1)}, f32[1,16,256,64]{2,3,1,0:T(8,128)}) conditional(s32[]{:T(128)} %bitcast.148, (f32[16,256]{1,0:T(8,128)}, f32[16,256]{1,0:T(8,128)S(1)}, f32[16,256,64]{1,2,0:T(8,128)}) %tuple.160, (s32[512]{0:T(512)S(1)}, s32[256]{0:T(256)S(1)}, bf16[2,256,16,64]{1,3,2,0:T(8,128)(2,1)}, ...), branch_computations={%region_8.8_spmd, %region_9.0_spmd} | conditional | flops 564797440 | bytes 43224172 | solution.py:85
  348.1 10.8 %conditional.5 = (f32[1,16,256]{2,1,0:T(8,128)}, f32[1,16,256]{2,1,0:T(8,128)S(1)}, f32[1,16,256,64]{2,3,1,0:T(8,128)S(1)}) conditional(s32[]{:T(128)} %bitcast.151, (f32[16,256]{1,0:T(8,128)}, f32[16,256]{1,0:T(8,128)S(1)}, f32[16,256,64]{1,2,0:T(8,128)S(1)}) %tuple.162, (s32[512]{0:T(512)S(1)}, s32[256]{0:T(256)S(1)}, ...), branch_computations={%region_4.4_spmd, %region_5.0_spmd} | conditional | flops 564797440 | bytes 34835508 | solution.py:85
  351.8 3.2 fusion.2
  361.6 11.9 %conditional.4 = (f32[1,16,256]{2,1,0:T(8,128)}, f32[1,16,256]{2,1,0:T(8,128)S(1)}, f32[1,16,256,64]{2,3,1,0:T(8,128)}) conditional(s32[]{:T(128)} %bitcast.148, (f32[16,256]{1,0:T(8,128)}, f32[16,256]{1,0:T(8,128)S(1)}, f32[16,256,64]{1,2,0:T(8,128)}) %tuple.160, (s32[512]{0:T(512)S(1)}, s32[256]{0:T(256)S(1)}, bf16[2,256,16,64]{1,3,2,0:T(8,128)(2,1)}, ...), branch_computations={%region_8.8_spmd, %region_9.0_spmd} | conditional | flops 564797440 | bytes 43224172 | solution.py:85
  365.3 3.2 fusion.20
  390.5 10.8 %conditional.5 = (f32[1,16,256]{2,1,0:T(8,128)}, f32[1,16,256]{2,1,0:T(8,128)S(1)}, f32[1,16,256,64]{2,3,1,0:T(8,128)S(1)}) conditional(s32[]{:T(128)} %bitcast.151, (f32[16,256]{1,0:T(8,128)}, f32[16,256]{1,0:T(8,128)S(1)}, f32[16,256,64]{1,2,0:T(8,128)S(1)}) %tuple.162, (s32[512]{0:T(512)S(1)}, s32[256]{0:T(256)S(1)}, ...), branch_computations={%region_4.4_spmd, %region_5.0_spmd} | conditional | flops 564797440 | bytes 34835508 | solution.py:85
  404.0 11.9 %conditional.4 = (f32[1,16,256]{2,1,0:T(8,128)}, f32[1,16,256]{2,1,0:T(8,128)S(1)}, f32[1,16,256,64]{2,3,1,0:T(8,128)}) conditional(s32[]{:T(128)} %bitcast.148, (f32[16,256]{1,0:T(8,128)}, f32[16,256]{1,0:T(8,128)S(1)}, f32[16,256,64]{1,2,0:T(8,128)}) %tuple.160, (s32[512]{0:T(512)S(1)}, s32[256]{0:T(256)S(1)}, bf16[2,256,16,64]{1,3,2,0:T(8,128)(2,1)}, ...), branch_computations={%region_8.8_spmd, %region_9.0_spmd} | conditional | flops 564797440 | bytes 43224172 | solution.py:85
  407.7 3.2 fusion.20
  435.7 11.9 %conditional.4 = (f32[1,16,256]{2,1,0:T(8,128)}, f32[1,16,256]{2,1,0:T(8,128)S(1)}, f32[1,16,256,64]{2,3,1,0:T(8,128)}) conditional(s32[]{:T(128)} %bitcast.148, (f32[16,256]{1,0:T(8,128)}, f32[16,256]{1,0:T(8,128)S(1)}, f32[16,256,64]{1,2,0:T(8,128)}) %tuple.160, (s32[512]{0:T(512)S(1)}, s32[256]{0:T(256)S(1)}, bf16[2,256,16,64]{1,3,2,0:T(8,128)(2,1)}, ...), branch_computations={%region_8.8_spmd, %region_9.0_spmd} | conditional | flops 564797440 | bytes 43224172 | solution.py:85
  439.4 3.2 fusion.20
  467.3 11.9 %conditional.4 = (f32[1,16,256]{2,1,0:T(8,128)}, f32[1,16,256]{2,1,0:T(8,128)S(1)}, f32[1,16,256,64]{2,3,1,0:T(8,128)}) conditional(s32[]{:T(128)} %bitcast.148, (f32[16,256]{1,0:T(8,128)}, f32[16,256]{1,0:T(8,128)S(1)}, f32[16,256,64]{1,2,0:T(8,128)}) %tuple.160, (s32[512]{0:T(512)S(1)}, s32[256]{0:T(256)S(1)}, bf16[2,256,16,64]{1,3,2,0:T(8,128)(2,1)}, ...), branch_computations={%region_8.8_spmd, %region_9.0_spmd} | conditional | flops 564797440 | bytes 43224172 | solution.py:85
  471.0 3.2 fusion.20
  498.9 11.9 %conditional.4 = (f32[1,16,256]{2,1,0:T(8,128)}, f32[1,16,256]{2,1,0:T(8,128)S(1)}, f32[1,16,256,64]{2,3,1,0:T(8,128)}) conditional(s32[]{:T(128)} %bitcast.148, (f32[16,256]{1,0:T(8,128)}, f32[16,256]{1,0:T(8,128)S(1)}, f32[16,256,64]{1,2,0:T(8,128)}) %tuple.160, (s32[512]{0:T(512)S(1)}, s32[256]{0:T(256)S(1)}, bf16[2,256,16,64]{1,3,2,0:T(8,128)(2,1)}, ...), branch_computations={%region_8.8_spmd, %region_9.0_spmd} | conditional | flops 564797440 | bytes 43224172 | solution.py:85
  502.7 3.2 fusion.20
  530.6 11.9 %conditional.4 = (f32[1,16,256]{2,1,0:T(8,128)}, f32[1,16,256]{2,1,0:T(8,128)S(1)}, f32[1,16,256,64]{2,3,1,0:T(8,128)}) conditional(s32[]{:T(128)} %bitcast.148, (f32[16,256]{1,0:T(8,128)}, f32[16,256]{1,0:T(8,128)S(1)}, f32[16,256,64]{1,2,0:T(8,128)}) %tuple.160, (s32[512]{0:T(512)S(1)}, s32[256]{0:T(256)S(1)}, bf16[2,256,16,64]{1,3,2,0:T(8,128)(2,1)}, ...), branch_computations={%region_8.8_spmd, %region_9.0_spmd} | conditional | flops 564797440 | bytes 43224172 | solution.py:85
  552.7 14.4 %collective-permute-done.1 = bf16[256,1024]{1,0:T(8,128)(2,1)S(1)} collective-permute-done((bf16[256,1024]{1,0:T(8,128)(2,1)S(1)}, bf16[256,1024]{1,0:T(8,128)(2,1)S(1)}, u32[]{:S(2)}, u32[]{:S(2)}) %collective-permute-start.1) | collective-permute-done | bytes 524320 | tf_op jit(solution)/shard_map/ppermute | solution.py:15
  (366 shorter events, 287.8 us)
Async XLA Ops:
  6.5 543.1 %copy-start = (bf16[1024,1024]{1,0:T(8,128)(2,1)S(1)}, bf16[1024,1024]{1,0:T(8,128)(2,1)}, u32[]{:S(2)}) copy-start(bf16[1024,1024]{1,0:T(8,128)(2,1)} %param.24) | copy-start | bytes 6291460
  6.5 52.6 %copy-start.13 = (bf16[1024]{0:T(1024)(128)(2,1)S(1)}, bf16[1024]{0:T(1024)(128)(2,1)}, u32[]{:S(2)}) copy-start(bf16[1024]{0:T(1024)(128)(2,1)} %param.20) | copy-start | bytes 6148
  48.5 27.7 %all-to-all-start.1 = ((bf16[32,1,128,128]{2,3,1,0:T(8,128)(2,1)}), bf16[32,1,128,128]{2,3,1,0:T(8,128)(2,1)S(1)}, u32[]{:S(2)}, u32[]{:S(2)}) async-start(bf16[32,1,128,128]{2,3,1,0:T(8,128)(2,1)} %constant_dynamic-update-slice_fusion), calls=%async_computation.1 | async-start | bytes 2097152 | tf_op jit(solution)/shard_map/all_to_all | solution.py:110
  59.1 177.6 %all-gather.2.cloned.1.call-start = ((), (), s32[]{:S(2)}) async-start(), calls=%async_computation.2 | async-start | bytes 17301504 | tf_op jit(solution)/shard_map/all_gather | solution.py:20
  76.2 5.4 copy-start.11
  81.1 4.9 copy-start.14
  85.1 28.6 %copy-start.6 = (bf16[256,1024]{1,0:T(8,128)(2,1)}, bf16[256,1024]{1,0:T(8,128)(2,1)S(1)}, u32[]{:S(2)}) copy-start(bf16[256,1024]{1,0:T(8,128)(2,1)S(1)} %get-tuple-element.363) | copy-start | bytes 1572868
  85.1 17.0 %collective-permute-start = (bf16[256,1024]{1,0:T(8,128)(2,1)}, bf16[256,1024]{1,0:T(8,128)(2,1)S(1)}, u32[]{:S(2)}, u32[]{:S(2)}) collective-permute-start(bf16[256,1024]{1,0:T(8,128)(2,1)} %get-tuple-element.364), channel_id=1, source_target_pairs={{0,16},{1,17},{2,18},{3,19},{4,20},{5,21},{6,22},{7,23},{8,24},{9,... | collective-permute-start | bytes 1572872 | tf_op jit(solution)/shard_map/ppermute | solution.py:15
  102.1 146.3 %copy-start.8 = (bf16[256,1024]{1,0:T(8,128)(2,1)}, bf16[256,1024]{1,0:T(8,128)(2,1)S(1)}, u32[]{:S(2)}) copy-start(bf16[256,1024]{1,0:T(8,128)(2,1)S(1)} %collective-permute-done) | copy-start | bytes 1572868
  263.4 7.5 %copy-start.4 = (bf16[512,16,64]{0,2,1:T(8,128)(2,1)S(1)}, bf16[512,16,64]{0,2,1:T(8,128)(2,1)}, u32[]{:S(2)}) copy-start(bf16[512,16,64]{0,2,1:T(8,128)(2,1)} %get-tuple-element.249) | copy-start | bytes 3145732 | tf_op jit(solution)/shard_map/while/body/eval_jaxpr/cond
  276.9 7.5 %copy-start.1 = (f32[16,256,64]{1,2,0:T(8,128)S(1)}, f32[16,256,64]{1,2,0:T(8,128)}, u32[]{:S(2)}) copy-start(f32[16,256,64]{1,2,0:T(8,128)} %get-tuple-element.256) | copy-start | bytes 3145732 | tf_op jit(solution)/shard_map/while/body/eval_jaxpr/cond
  276.9 7.5 %copy-start.5 = (bf16[512,16,64]{0,2,1:T(8,128)(2,1)S(1)}, bf16[512,16,64]{0,2,1:T(8,128)(2,1)}, u32[]{:S(2)}) copy-start(bf16[512,16,64]{0,2,1:T(8,128)(2,1)} %get-tuple-element.257) | copy-start | bytes 3145732 | tf_op jit(solution)/shard_map/while/body/eval_jaxpr/cond
  305.8 7.5 %copy-start.4 = (bf16[512,16,64]{0,2,1:T(8,128)(2,1)S(1)}, bf16[512,16,64]{0,2,1:T(8,128)(2,1)}, u32[]{:S(2)}) copy-start(bf16[512,16,64]{0,2,1:T(8,128)(2,1)} %get-tuple-element.249) | copy-start | bytes 3145732 | tf_op jit(solution)/shard_map/while/body/eval_jaxpr/cond
  319.3 7.5 %copy-start.1 = (f32[16,256,64]{1,2,0:T(8,128)S(1)}, f32[16,256,64]{1,2,0:T(8,128)}, u32[]{:S(2)}) copy-start(f32[16,256,64]{1,2,0:T(8,128)} %get-tuple-element.256) | copy-start | bytes 3145732 | tf_op jit(solution)/shard_map/while/body/eval_jaxpr/cond
  319.3 7.5 %copy-start.5 = (bf16[512,16,64]{0,2,1:T(8,128)(2,1)S(1)}, bf16[512,16,64]{0,2,1:T(8,128)(2,1)}, u32[]{:S(2)}) copy-start(bf16[512,16,64]{0,2,1:T(8,128)(2,1)} %get-tuple-element.257) | copy-start | bytes 3145732 | tf_op jit(solution)/shard_map/while/body/eval_jaxpr/cond
  348.3 7.5 %copy-start.4 = (bf16[512,16,64]{0,2,1:T(8,128)(2,1)S(1)}, bf16[512,16,64]{0,2,1:T(8,128)(2,1)}, u32[]{:S(2)}) copy-start(bf16[512,16,64]{0,2,1:T(8,128)(2,1)} %get-tuple-element.249) | copy-start | bytes 3145732 | tf_op jit(solution)/shard_map/while/body/eval_jaxpr/cond
  361.7 7.5 %copy-start.1 = (f32[16,256,64]{1,2,0:T(8,128)S(1)}, f32[16,256,64]{1,2,0:T(8,128)}, u32[]{:S(2)}) copy-start(f32[16,256,64]{1,2,0:T(8,128)} %get-tuple-element.256) | copy-start | bytes 3145732 | tf_op jit(solution)/shard_map/while/body/eval_jaxpr/cond
  361.8 7.5 %copy-start.5 = (bf16[512,16,64]{0,2,1:T(8,128)(2,1)S(1)}, bf16[512,16,64]{0,2,1:T(8,128)(2,1)}, u32[]{:S(2)}) copy-start(bf16[512,16,64]{0,2,1:T(8,128)(2,1)} %get-tuple-element.257) | copy-start | bytes 3145732 | tf_op jit(solution)/shard_map/while/body/eval_jaxpr/cond
  390.7 7.5 %copy-start.4 = (bf16[512,16,64]{0,2,1:T(8,128)(2,1)S(1)}, bf16[512,16,64]{0,2,1:T(8,128)(2,1)}, u32[]{:S(2)}) copy-start(bf16[512,16,64]{0,2,1:T(8,128)(2,1)} %get-tuple-element.249) | copy-start | bytes 3145732 | tf_op jit(solution)/shard_map/while/body/eval_jaxpr/cond
  404.2 7.5 %copy-start.1 = (f32[16,256,64]{1,2,0:T(8,128)S(1)}, f32[16,256,64]{1,2,0:T(8,128)}, u32[]{:S(2)}) copy-start(f32[16,256,64]{1,2,0:T(8,128)} %get-tuple-element.256) | copy-start | bytes 3145732 | tf_op jit(solution)/shard_map/while/body/eval_jaxpr/cond
  404.2 7.5 %copy-start.5 = (bf16[512,16,64]{0,2,1:T(8,128)(2,1)S(1)}, bf16[512,16,64]{0,2,1:T(8,128)(2,1)}, u32[]{:S(2)}) copy-start(bf16[512,16,64]{0,2,1:T(8,128)(2,1)} %get-tuple-element.257) | copy-start | bytes 3145732 | tf_op jit(solution)/shard_map/while/body/eval_jaxpr/cond
  435.8 7.5 %copy-start.1 = (f32[16,256,64]{1,2,0:T(8,128)S(1)}, f32[16,256,64]{1,2,0:T(8,128)}, u32[]{:S(2)}) copy-start(f32[16,256,64]{1,2,0:T(8,128)} %get-tuple-element.256) | copy-start | bytes 3145732 | tf_op jit(solution)/shard_map/while/body/eval_jaxpr/cond
  435.8 7.5 %copy-start.5 = (bf16[512,16,64]{0,2,1:T(8,128)(2,1)S(1)}, bf16[512,16,64]{0,2,1:T(8,128)(2,1)}, u32[]{:S(2)}) copy-start(bf16[512,16,64]{0,2,1:T(8,128)(2,1)} %get-tuple-element.257) | copy-start | bytes 3145732 | tf_op jit(solution)/shard_map/while/body/eval_jaxpr/cond
  467.5 7.5 %copy-start.1 = (f32[16,256,64]{1,2,0:T(8,128)S(1)}, f32[16,256,64]{1,2,0:T(8,128)}, u32[]{:S(2)}) copy-start(f32[16,256,64]{1,2,0:T(8,128)} %get-tuple-element.256) | copy-start | bytes 3145732 | tf_op jit(solution)/shard_map/while/body/eval_jaxpr/cond
  467.5 7.5 %copy-start.5 = (bf16[512,16,64]{0,2,1:T(8,128)(2,1)S(1)}, bf16[512,16,64]{0,2,1:T(8,128)(2,1)}, u32[]{:S(2)}) copy-start(bf16[512,16,64]{0,2,1:T(8,128)(2,1)} %get-tuple-element.257) | copy-start | bytes 3145732 | tf_op jit(solution)/shard_map/while/body/eval_jaxpr/cond
  499.1 7.5 %copy-start.1 = (f32[16,256,64]{1,2,0:T(8,128)S(1)}, f32[16,256,64]{1,2,0:T(8,128)}, u32[]{:S(2)}) copy-start(f32[16,256,64]{1,2,0:T(8,128)} %get-tuple-element.256) | copy-start | bytes 3145732 | tf_op jit(solution)/shard_map/while/body/eval_jaxpr/cond
  499.1 7.5 %copy-start.5 = (bf16[512,16,64]{0,2,1:T(8,128)(2,1)S(1)}, bf16[512,16,64]{0,2,1:T(8,128)(2,1)}, u32[]{:S(2)}) copy-start(bf16[512,16,64]{0,2,1:T(8,128)(2,1)} %get-tuple-element.257) | copy-start | bytes 3145732 | tf_op jit(solution)/shard_map/while/body/eval_jaxpr/cond
  530.8 7.5 %copy-start.1 = (f32[16,256,64]{1,2,0:T(8,128)S(1)}, f32[16,256,64]{1,2,0:T(8,128)}, u32[]{:S(2)}) copy-start(f32[16,256,64]{1,2,0:T(8,128)} %get-tuple-element.256) | copy-start | bytes 3145732 | tf_op jit(solution)/shard_map/while/body/eval_jaxpr/cond
  530.8 7.5 %copy-start.5 = (bf16[512,16,64]{0,2,1:T(8,128)(2,1)S(1)}, bf16[512,16,64]{0,2,1:T(8,128)(2,1)}, u32[]{:S(2)}) copy-start(bf16[512,16,64]{0,2,1:T(8,128)(2,1)} %get-tuple-element.257) | copy-start | bytes 3145732 | tf_op jit(solution)/shard_map/while/body/eval_jaxpr/cond
  546.3 5.9 %copy-start.7 = (bf16[256,1024]{1,0:T(8,128)(2,1)S(1)}, bf16[256,1024]{1,0:T(8,128)(2,1)}, u32[]{:S(2)}) copy-start(bf16[256,1024]{1,0:T(8,128)(2,1)} %copy-done.6) | copy-start | bytes 1572868
  546.3 5.9 %copy-start.9 = (bf16[256,1024]{1,0:T(8,128)(2,1)S(1)}, bf16[256,1024]{1,0:T(8,128)(2,1)}, u32[]{:S(2)}) copy-start(bf16[256,1024]{1,0:T(8,128)(2,1)} %copy-done.8) | copy-start | bytes 1572868
  552.6 14.5 %collective-permute-start.1 = (bf16[256,1024]{1,0:T(8,128)(2,1)S(1)}, bf16[256,1024]{1,0:T(8,128)(2,1)S(1)}, u32[]{:S(2)}, u32[]{:S(2)}) collective-permute-start(bf16[256,1024]{1,0:T(8,128)(2,1)S(1)} %get-tuple-element.362), channel_id=1, source_target_pairs={{0,16},{1,17},{2,18},{3,19},{4,20},{5,21},{6,22},{7,23},{8,24},{9,... | collective-permute-start | bytes 1572872 | tf_op jit(solution)/shard_map/ppermute | solution.py:15
  (18 other events, 38.8 us)
Sparse Core Ops, SparseCore 0:
  83.1 153.5 all-gather.1
